TPU v7x, 32 devices: a whole 2x2x4 slice. The times are simulated.
32 devices in a mesh: slab: 32 (over z, y, x, core).
Axes of the slice: x: 2, y: 2, z: 4, core: 2. Of those that a mesh axis runs over, the one named last changes fastest.
Arguments:
- points: float32 [4, 128, 128, 64], P(None, 'slab'), may hold values from -6 to 6
- offsets_x: int32 [256], replicated, may hold values from 0 to 124, as said below
- coeffs_x: float32 [4, 256], replicated, may hold values from 0.1 to 1
- offsets_y: int32 [256], replicated, may hold values from 0 to 124, as said below
- coeffs_y: float32 [4, 256], replicated, may hold values from 0.1 to 1
- offsets_z: int32 [128], replicated, may hold values from 0 to 60, as said below
- coeffs_z: float32 [4, 128], replicated, may hold values from 0.1 to 1
Outputs:
- refined: float32 [4, 256, 256, 128], P(None, None, 'slab')
Inputs may be any that keep to these rules, and one draw needn't show every extreme that they name: offsets_x[i] lies between i // 2 - 2 and i // 2, clipped to 0 .. 124. offsets_y[i] lies between i // 2 - 2 and i // 2, clipped to 0 .. 124. offsets_z[i] lies between i // 2 - 2 and i // 2, clipped to 0 .. 60.
All inputs are finite; a program needn't handle non-finite values.
Results may differ from a plain program's by a relative error of at most 0.000073.
Values sent between devices are 32-bit elements; how exact they have to be, the bound alone decides.
A program may use at most 64 MiB of HBM per device.

v0:
```python
import functools

import jax
import jax.numpy as jnp
from jax import lax
from jax.experimental import pallas as pl
from jax.experimental.pallas import tpu as pltpu
from jax.sharding import PartitionSpec as P

MESH = pl.DeviceIdType.MESH
BAND = 4
REACH = BAND + 1
SPAN = BAND + 2
BELOW, ABOVE = 2, 3
PLANES = 4
GROUP = 8


def flip(a, k, chips):
    out = 0
    bit = 1
    while bit < chips:
        a_bit, k_bit = (a // bit) % 2, (k // bit) % 2
        out = out + (a_bit + k_bit - 2 * a_bit * k_bit) * bit
        bit *= 2
    return out


def span_of(me, jl, ny, j):
    return jnp.clip((me * jl + j) // 2 - 2, 0, ny - SPAN)


def make_weights(dims, me, span_base, oy_ref, cy_ref, oz_ref, cz_ref, cx_ref, wx_ref, wy, rz, rz_lo):
    n, comps, xl, ny, nz, jl, mz = dims
    pairs, lanes = wy.shape[1], wy.shape[2]
    fold = lanes // nz
    wx_ref[...] = cx_ref[...] / jnp.sum(cx_ref[...], axis=0, keepdims=True)
    wz = cz_ref[...] / jnp.sum(cz_ref[...], axis=0, keepdims=True)
    at = lax.broadcasted_iota(jnp.int32, (nz, mz), 0)
    first = jnp.broadcast_to(oz_ref[...], (nz, mz))
    band = jnp.zeros((nz, mz), jnp.float32)
    for k in range(BAND):
        band = band + jnp.where(at == first + k, jnp.broadcast_to(wz[k : k + 1], (nz, mz)), 0.0)
    high = band.astype(jnp.bfloat16)
    low = (band - high.astype(jnp.float32)).astype(jnp.bfloat16)
    rz[...] = jnp.zeros_like(rz)
    rz_lo[...] = jnp.zeros_like(rz_lo)
    for f in range(fold):
        rz[f * nz : (f + 1) * nz, f * mz : (f + 1) * mz] = high
        rz[lanes + f * nz : lanes + (f + 1) * nz, f * mz : (f + 1) * mz] = high
        rz_lo[f * nz : (f + 1) * nz, f * mz : (f + 1) * mz] = low
    for j in range(jl):
        coeffs = [jnp.full((pairs, lanes), cy_ref[k, me * jl + j]) for k in range(BAND)]
        total = coeffs[0] + coeffs[1] + coeffs[2] + coeffs[3]
        coeffs = [c / total for c in coeffs]
        skip = jnp.full((pairs, lanes), oy_ref[me * jl + j] - span_base(j))
        for m in range(SPAN):
            weight = jnp.zeros((pairs, lanes), jnp.float32)
            for k in range(max(0, m - SPAN + BAND), min(BAND, m + 1)):
                weight = jnp.where(skip == m - k, coeffs[k], weight)
            wy[j * SPAN + m] = weight


def refine_y(jl, pairs, span_base, wy, mixed, place, load, base):
    for j in range(jl):
        row = span_base(j) - base
        acc = wy[j * SPAN] * load(row)
        for m in range(1, SPAN):
            acc = acc + wy[j * SPAN + m] * load(row + m)
        mixed[pl.ds(place * pairs * jl + j, pairs, stride=jl), :] = acc


def refine_z(dims, pairs, mixed, rz, rz_lo, grid_ref, devices):
    n, comps, xl, ny, nz, jl, mz = dims
    fold = mixed.shape[1] // nz
    rows = pairs * jl * len(devices)
    x = mixed[:rows]
    hi = x.astype(jnp.bfloat16)
    lo = (x - hi.astype(jnp.float32)).astype(jnp.bfloat16)
    both = jnp.concatenate([hi, lo], axis=1)
    res = jnp.dot(both, rz[...], preferred_element_type=jnp.float32)
    res = res + jnp.dot(hi, rz_lo[...], preferred_element_type=jnp.float32)
    per = pairs // comps
    for q, device in enumerate(devices):
        for p in range(pairs):
            for f in range(fold):
                spot = (p // per, device * xl + (p % per) * fold + f)
                top = (q * pairs + p) * jl
                grid_ref[spot] = res[top : top + jl, f * mz : (f + 1) * mz]


def exchange(
    dims,
    points_ref, oy_ref, cy_ref, oz_ref, cz_ref, cx_ref,
    grid_ref, wx_ref,
    send, direct, passed, wy, rz, rz_lo, mixed,
    send_sem, recv_sem, pass_send_sem, pass_recv_sem,
):
    n, comps, xl, ny, nz, jl, mz = dims
    chips = n // 2
    pairs, lanes = points_ref.shape[0], points_ref.shape[1]
    cl = jl // 2
    wide, narrow = 2 * cl + REACH, cl + REACH
    me = lax.axis_index("slab")
    chip, core = me // 2, me % 2
    partner = chip * 2 + 1 - core

    def wide_base(c):
        return jnp.clip(c * 2 * cl - 2, 0, ny - wide)

    def narrow_base(d):
        return jnp.clip(d * cl - 2, 0, ny - narrow)

    span_base = functools.partial(span_of, me, jl, ny)

    rows_of_y = send.reshape(ny, pairs, lanes)

    barrier = pltpu.get_barrier_semaphore()
    pl.semaphore_signal(barrier, inc=1, device_id=(partner,), device_id_type=MESH)

    @pl.loop(1, chips)
    def _(k):
        other = flip(chip, k, chips) * 2 + core
        pl.semaphore_signal(barrier, inc=1, device_id=(other,), device_id_type=MESH)

    for p in range(pairs):
        send[pl.ds(p, ny, stride=pairs), :] = points_ref[p].T

    pl.semaphore_wait(barrier, chips)

    def out_copy(k):
        target = flip(chip, k, chips)
        return pltpu.make_async_remote_copy(
            src_ref=rows_of_y.at[pl.ds(wide_base(target), wide)],
            dst_ref=direct.at[k],
            send_sem=send_sem.at[k],
            recv_sem=recv_sem.at[k],
            device_id=(target * 2 + core,),
            device_id_type=MESH,
        )

    def pass_copy(k):
        skip = narrow_base(partner) - wide_base(chip)
        return pltpu.make_async_remote_copy(
            src_ref=direct.at[k, pl.ds(skip, narrow)],
            dst_ref=passed.at[k],
            send_sem=pass_send_sem.at[k],
            recv_sem=pass_recv_sem.at[k],
            device_id=(partner,),
            device_id_type=MESH,
        )

    @pl.loop(1, chips)
    def _(k):
        out_copy(k).start()

    own = pl.ds(wide_base(chip), wide)
    stay = pltpu.make_async_copy(rows_of_y.at[own], direct.at[0], recv_sem.at[0])
    stay.start()

    make_weights(dims, me, span_base, oy_ref, cy_ref, oz_ref, cz_ref, cx_ref, wx_ref, wy, rz, rz_lo)

    def from_direct(place, k):
        refine_y(
            jl, pairs, span_base, wy, mixed, place,
            lambda row: direct[k, row],
            wide_base(chip),
        )
        return flip(chip, k, chips) * 2 + core

    def from_passed(place, k):
        refine_y(
            jl, pairs, span_base, wy, mixed, place,
            lambda row: passed[k, row],
            narrow_base(me),
        )
        return flip(chip, k, chips) * 2 + 1 - core

    stay.wait()
    pass_copy(0).start()
    refine_z(dims, pairs, mixed, rz, rz_lo, grid_ref, [from_direct(0, 0)])

    @pl.loop(1, chips)
    def _(k):
        out_copy(k).wait_recv()
        pass_copy(k).start()
        one = from_direct(0, k)
        pass_copy(k - 1).wait_recv()
        two = from_passed(1, k - 1)
        refine_z(dims, pairs, mixed, rz, rz_lo, grid_ref, [one, two])

    pass_copy(chips - 1).wait_recv()
    refine_z(dims, pairs, mixed, rz, rz_lo, grid_ref, [from_passed(0, chips - 1)])

    @pl.loop(1, chips)
    def _(k):
        out_copy(k).wait_send()

    @pl.loop(0, chips)
    def _(k):
        pass_copy(k).wait_send()


def relay(
    dims,
    points_ref, oy_ref, cy_ref, oz_ref, cz_ref, cx_ref,
    grid_ref, wx_ref,
    send, held, wy, rz, rz_lo, mixed,
    main_send, main_recv, pass_send, pass_recv, up_send, down_send, halo_recv, edge_send,
):
    n, comps, xl, ny, nz, jl, mz = dims
    chips = n // 2
    plane = chips // PLANES
    pairs, lanes = points_ref.shape[0], points_ref.shape[1]
    own = jl
    me = lax.axis_index("slab")
    chip, core = me // 2, me % 2
    partner = chip * 2 + 1 - core
    here, level = chip % plane, chip // plane
    middle = pl.ds(BELOW, own)
    rows_of_y = send.reshape(ny, pairs, lanes)

    barrier = pltpu.get_barrier_semaphore()

    @pl.loop(1, n)
    def _(k):
        pl.semaphore_signal(barrier, inc=1, device_id=((me + k) % n,), device_id_type=MESH)

    for p in range(pairs):
        send[pl.ds(p, ny, stride=pairs), :] = points_ref[p].T
    span_base = functools.partial(span_of, me, jl, ny)
    make_weights(dims, me, span_base, oy_ref, cy_ref, oz_ref, cz_ref, cx_ref, wx_ref, wy, rz, rz_lo)
    held[me, middle] = rows_of_y[pl.ds(chip * own, own)]

    pl.semaphore_wait(barrier, n - 1)

    def remote(src, dst, send_sem, recv_sem, device):
        return pltpu.make_async_remote_copy(
            src_ref=src, dst_ref=dst, send_sem=send_sem, recv_sem=recv_sem,
            device_id=(device,), device_id_type=MESH,
        )

    def main_copy(k):
        target = flip(chip, k, chips)
        return remote(
            rows_of_y.at[pl.ds(target * own, own)], held.at[me, middle],
            main_send.at[k], main_recv.at[k], target * 2 + core,
        )

    def main_arrival(k):
        source = flip(chip, k, chips) * 2 + core
        return remote(held.at[source, middle], held.at[source, middle], main_send.at[k], main_recv.at[k], partner)

    def pass_copy(k):
        source = flip(chip, k, chips) * 2 + core
        return remote(held.at[source, middle], held.at[source, middle], pass_send.at[k], pass_recv.at[k], partner)

    def pass_arrival(k):
        source = flip(chip, k, chips) * 2 + 1 - core
        return remote(held.at[source, middle], held.at[source, middle], pass_send.at[k], pass_recv.at[k], partner)

    def up_copy(k):
        source = flip(chip, k, chips) * 2 + core
        return remote(
            held.at[source, pl.ds(own, BELOW)], held.at[source, pl.ds(0, BELOW)],
            up_send.at[k], halo_recv.at[source], chip * 2 + 2,
        )

    def down_copy(k):
        source = flip(chip, k, chips) * 2 + core
        return remote(
            held.at[source, pl.ds(BELOW, ABOVE)], held.at[source, pl.ds(BELOW + own, ABOVE)],
            down_send.at[k], halo_recv.at[source], chip * 2 - 1,
        )

    has_up = here < plane - 1
    has_down = here > 0

    def edge_below(g):
        target = flip(level, g, PLANES) * plane
        copy = lambda: remote(
            rows_of_y.at[pl.ds(target * own - BELOW, BELOW)], held.at[me, pl.ds(0, BELOW)],
            edge_send.at[g], halo_recv.at[me], target * 2,
        )
        return (target > 0) & (target * 2 != me), copy

    def edge_above(g):
        target = flip(level, g, PLANES) * plane + plane - 1
        copy = lambda: remote(
            rows_of_y.at[pl.ds(target * own + own, ABOVE)], held.at[me, pl.ds(BELOW + own, ABOVE)],
            edge_send.at[PLANES + g], halo_recv.at[me], target * 2 + 1,
        )
        return (target < chips - 1) & (target * 2 + 1 != me), copy

    def send_edges(g):
        for edge in (edge_below, edge_above):
            needed, copy = edge(g)

            @pl.when(needed)
            def _():
                copy().start()

    def hand_on(k):
        pass_copy(k).start()

        @pl.when(has_up)
        def _():
            up_copy(k).start()

        @pl.when(has_down)
        def _():
            down_copy(k).start()

    @pl.loop(1, plane)
    def _(k):
        main_copy(k).start()

    send_edges(0)
    hand_on(0)

    for g in range(1, PLANES):

        @pl.loop(g * plane, (g + 1) * plane)
        def _(k):
            main_copy(k).start()

        send_edges(g)

    at_bottom = (here == 0) & (core == 0)
    at_top = (here == plane - 1) & (core == 1)

    @pl.when(at_bottom & (chip > 0))
    def _():
        held[me, 0:BELOW] = rows_of_y[pl.ds(chip * own - BELOW, BELOW)]

    @pl.when(at_top & (chip < chips - 1))
    def _():
        held[me, BELOW + own :] = rows_of_y[pl.ds(chip * own + own, ABOVE)]

    def await_halo(source):
        away = (source != me) | ((here != 0) & (core == 0)) | ((here != plane - 1) & (core == 1))

        @pl.when(away & (core == 0) & (chip > 0))
        def _():
            rows = held.at[source, pl.ds(0, BELOW)]
            remote(rows, rows, up_send.at[0], halo_recv.at[source], partner).wait_recv()

        @pl.when(away & (core == 1) & (chip < chips - 1))
        def _():
            rows = held.at[source, pl.ds(BELOW + own, ABOVE)]
            remote(rows, rows, up_send.at[0], halo_recv.at[source], partner).wait_recv()

    def refine(k):
        others = [flip(chip, k + i, chips) * 2 for i in range(2)]
        for i in range(2):
            pass_arrival(k + i).wait_recv()
        devices = [other + c for other in others for c in range(2)]
        for device in devices:
            await_halo(device)
        for j in range(jl):
            row = span_base(j) - (chip * own - BELOW)
            sums = [None] * len(devices)
            for m in range(SPAN):
                weight = wy[j * SPAN + m]
                for i, device in enumerate(devices):
                    term = weight * held[device, row + m]
                    sums[i] = term if m == 0 else sums[i] + term
            for i, total in enumerate(sums):
                mixed[pl.ds(i * pairs * jl + j, pairs, stride=jl), :] = total
        refine_z(dims, pairs, mixed, rz, rz_lo, grid_ref, devices)

    def take(k):
        main_arrival(k).wait_recv()
        hand_on(k)

    @pl.loop(1, plane)
    def _(k):
        take(k)

    @pl.loop(1, PLANES)
    def _(g):
        @pl.loop(0, plane)
        def _(r):
            take(g * plane + r)

        @pl.loop(0, plane // 2)
        def _(h):
            refine((g - 1) * plane + 2 * h)

    @pl.loop((chips - plane) // 2, chips // 2)
    def _(h):
        refine(2 * h)

    @pl.loop(1, chips)
    def _(k):
        main_copy(k).wait_send()

    @pl.loop(0, chips)
    def _(k):
        pass_copy(k).wait_send()

        @pl.when(has_up)
        def _():
            up_copy(k).wait_send()

        @pl.when(has_down)
        def _():
            down_copy(k).wait_send()

    for g in range(PLANES):
        for edge in (edge_below, edge_above):
            needed, copy = edge(g)

            @pl.when(needed)
            def _():
                copy().wait_send()


def refine_x(steps, ox_ref, wx_ref, grid_ref, out_ref, block, sems):
    comps, mx = block.shape[0], block.shape[1]
    rows = mx // steps

    def put(s):
        part = pl.ds(pl.multiple_of(s * rows, rows), rows)
        return pltpu.make_async_copy(block.at[:, part], out_ref.at[:, part], sems.at[s])

    @pl.loop(0, steps)
    def _(s):
        @pl.loop(0, rows // GROUP)
        def _(g):
            done = []
            for q in range(GROUP):
                i = s * rows + g * GROUP + q
                first = ox_ref[i]
                weights = [wx_ref[k, i] for k in range(BAND)]
                for c in range(comps):
                    acc = weights[0] * grid_ref[c, first]
                    for k in range(1, BAND):
                        acc = acc + weights[k] * grid_ref[c, first + k]
                    done.append((c, i, acc))
            for c, i, acc in done:
                block[c, i] = acc

        put(s).start()

    @pl.loop(0, steps)
    def _(s):
        put(s).wait()


def solution(mesh):
    n = mesh.shape["slab"]
    vmem = pl.BlockSpec(memory_space=pltpu.VMEM)
    smem = pl.BlockSpec(memory_space=pltpu.SMEM)

    def body(points, offsets_x, coeffs_x, offsets_y, coeffs_y, offsets_z, coeffs_z):
        comps, xl, ny, nz = points.shape
        nx = xl * n
        mx, my, mz = offsets_x.shape[0], offsets_y.shape[0], offsets_z.shape[0]
        jl = my // n
        fold = 128 // nz
        pairs = comps * xl // fold
        lanes = fold * nz
        chips = n // 2
        cl = jl // 2
        wide, narrow = 2 * cl + REACH, cl + REACH
        slab = jnp.transpose(points, (0, 1, 3, 2)).reshape(pairs, lanes, ny)
        f32, bf16 = jnp.float32, jnp.bfloat16
        if jl >= ABOVE and chips % PLANES == 0:
            kernel, name = relay, "relay"
            buffers = [pltpu.VMEM((n, BELOW + jl + ABOVE, pairs, lanes), f32)]
            counts = [chips] * 6 + [n, 2 * PLANES]
        else:
            kernel, name = exchange, "exchange"
            buffers = [
                pltpu.VMEM((chips, wide, pairs, lanes), f32),
                pltpu.VMEM((chips, narrow, pairs, lanes), f32),
            ]
            counts = [chips] * 4
        grid, wx = pl.pallas_call(
            functools.partial(kernel, (n, comps, xl, ny, nz, jl, mz)),
            out_shape=(
                pltpu.VMEM((comps, nx, jl, mz), f32),
                jax.ShapeDtypeStruct((BAND, mx), f32),
            ),
            in_specs=[vmem, smem, smem, vmem, vmem, vmem],
            out_specs=(vmem, vmem),
            scratch_shapes=[
                pltpu.VMEM((ny * pairs, lanes), f32),
                *buffers,
                pltpu.VMEM((jl * SPAN, pairs, lanes), f32),
                pltpu.VMEM((2 * lanes, fold * mz), bf16),
                pltpu.VMEM((lanes, fold * mz), bf16),
                pltpu.VMEM((4 * pairs * jl, lanes), f32),
                *[pltpu.SemaphoreType.DMA((count,)) for count in counts],
            ],
            compiler_params=pltpu.CompilerParams(collective_id=0, has_side_effects=True),
            name=name,
        )(slab, offsets_y, coeffs_y, offsets_z.reshape(1, mz), coeffs_z, coeffs_x)
        steps = 8
        return pl.pallas_call(
            functools.partial(refine_x, steps),
            out_shape=jax.ShapeDtypeStruct((comps, mx, jl, mz), f32),
            in_specs=[smem, smem, vmem],
            out_specs=pl.BlockSpec(memory_space=pltpu.HBM),
            scratch_shapes=[
                pltpu.VMEM((comps, mx, jl, mz), f32),
                pltpu.SemaphoreType.DMA((steps,)),
            ],
            name="refine_x",
        )(offsets_x, wx, pltpu.with_memory_space_constraint(grid, pltpu.VMEM))

    return jax.shard_map(
        body,
        mesh=mesh,
        in_specs=(P(None, "slab", None, None), P(), P(), P(), P(), P(), P()),
        out_specs=P(None, None, "slab", None),
        check_vma=False,
    )
```

profile of v0, /device:TPU:11, one launch (start us, length us, event | category | flops | bytes accessed | tf_op | source)
XLA Modules:
  0.0 29.0 jit_solution(17154303536550822255)
XLA Ops:
  0.0 25.8 %relay.1 = (f32[4,128,8,128]{3,2,1,0:T(8,128)S(1)}, f32[4,256]{1,0:T(4,128)}) custom-call(f32[8,128,128]{2,1,0:T(8,128)} %bitcast.4, s32[256]{0:T(256)} %oy_ref.1, f32[4,256]{1,0:T(4,128)} %cy_ref.1, s32[1,128]{1,0:T(1,128)} %bitcast.5, f32[4,128]{1,0:T(4,128)} %cz_ref.1, f32[4,256]{1,0:T(4,128)} %cx_ref.1), custom_call_target="tpu_custom_call" | custom-call | tf_op jit(solution)/shard_map/relay/pallas_call | solution.py:480
  25.8 3.2 %refine_x.1 = f32[4,256,8,128]{3,2,1,0:T(8,128)} custom-call(s32[256]{0:T(256)} %ox_ref.1, f32[4,256]{1,0:T(4,128)} %get-tuple-element.7.wx_ref, f32[4,128,8,128]{3,2,1,0:T(8,128)S(1)} %get-tuple-element.8.grid_ref), custom_call_target="tpu_custom_call" | custom-call | tf_op jit(solution)/shard_map/refine_x/pallas_call | solution.py:501
where the time goes:
time: 29.2 us; the launch traced here: 29 us
  Pallas kernels  29 us (99%)
    pallas_call x1, Pallas kernels, body(): pl.pallas_call(functools.partial(kernel, (n, comps, xl, ny, nz, jl, mz)),...  25.8 us
    pallas_call x1, Pallas kernels, body(): pl.pallas_call(functools.partial(refine_x, steps), out_shape=jax.ShapeDty...  3.19 us

commit v1 on v0

--- a/solution.py
+++ b/solution.py
@@ -14,13 +14,14 @@
 BELOW, ABOVE = 2, 3
 PLANES = 4
 GROUP = 8
+VMEM_MOST = 67043328
 
 
 def flip(a, k, chips):
     out = 0
     bit = 1
     while bit < chips:
-        a_bit, k_bit = (a // bit) % 2, (k // bit) % 2
+        a_bit, k_bit = lax.rem(lax.div(a, bit), 2), (k // bit) % 2
         out = out + (a_bit + k_bit - 2 * a_bit * k_bit) * bit
         bit *= 2
     return out
@@ -203,36 +204,109 @@
 
 def relay(
     dims,
-    points_ref, oy_ref, cy_ref, oz_ref, cz_ref, cx_ref,
-    grid_ref, wx_ref,
-    send, held, wy, rz, rz_lo, mixed,
-    main_send, main_recv, pass_send, pass_recv, up_send, down_send, halo_recv, edge_send,
+    points_hbm, oy_hbm, cy_hbm, oz_hbm, cz_hbm, cx_hbm, ox_hbm,
+    block_ref,
+    slab, send, direct, passed, wy, rz, rz_lo, mixed,
+    oy_ref, cy_ref, oz_ref, cz_ref, cx_ref,
+    grid_ref, ox_ref, wx_ref, wx_scalars,
+    load_sem, small_sem, out_sem, hand_sem, pass_sem,
+    whole_recv, low_recv, high_recv, middle_recv, pass_recv,
+    flags, partner_flag,
 ):
     n, comps, xl, ny, nz, jl, mz = dims
     chips = n // 2
     plane = chips // PLANES
-    pairs, lanes = points_ref.shape[0], points_ref.shape[1]
-    own = jl
+    pairs, lanes = slab.shape[0], slab.shape[1]
+    own, half = jl, jl // 2
+    wide, narrow = own + REACH, half + REACH
+    whole, low, high = pl.ds(0, wide), pl.ds(0, REACH), pl.ds(own, REACH)
+    middle = pl.ds(REACH, own - REACH)
     me = lax.axis_index("slab")
-    chip, core = me // 2, me % 2
+    chip, core = lax.div(me, 2), lax.rem(me, 2)
     partner = chip * 2 + 1 - core
-    here, level = chip % plane, chip // plane
-    middle = pl.ds(BELOW, own)
-    rows_of_y = send.reshape(ny, pairs, lanes)
+    here, level = lax.rem(chip, plane), lax.div(chip, plane)
+    rows_of_y = send.reshape(ny + REACH, pairs, lanes)
+    any_rows = direct.reshape(PLANES * plane * wide, pairs, lanes)
+    span_base = functools.partial(span_of, me, jl, ny)
+    around = [flip(here, d, plane) for d in range(plane)]
+
+    loads = [pltpu.make_async_copy(points_hbm.at[p], slab.at[p], load_sem.at[p]) for p in range(pairs)]
+    for load in loads:
+        load.start()
 
     barrier = pltpu.get_barrier_semaphore()
 
-    @pl.loop(1, n)
-    def _(k):
-        pl.semaphore_signal(barrier, inc=1, device_id=((me + k) % n,), device_id_type=MESH)
-
+    def greet(semaphore, device):
+        pl.semaphore_signal(semaphore, inc=1, device_id=(device,), device_id_type=MESH)
+
+    def device_of(z, q):
+        return (z * plane + q) * 2 + core
+
+    side = [lax.rem(here, 2), lax.div(here, 2)]
+    above = [None, side[0] == 0, side[1] == 0, side[0] + side[1] == 0]
+    below = [None, side[0] == 1, side[1] == 1, side[0] + side[1] == 2]
+    missing = [None, side[0] == 0, side[1] == 0, side[0] + side[1] < 2]
+
+    @pl.when(core == 0)
+    def _():
+        greet(barrier, partner)
+
+    for d in range(plane):
+        def hail(d=d):
+            @pl.loop(level + (d == 0), PLANES)
+            def _(z):
+                greet(barrier, device_of(z, around[d]))
+
+        hail() if d == 0 else pl.when(above[d])(hail)
+
+    smalls = [
+        pltpu.make_async_copy(src, dst, small_sem.at[i])
+        for i, (src, dst) in enumerate(
+            [(oy_hbm, oy_ref), (cy_hbm, cy_ref), (oz_hbm, oz_ref), (cz_hbm, cz_ref), (cx_hbm, cx_ref), (ox_hbm, ox_ref)]
+        )
+    ]
+    for small in smalls:
+        small.start()
+
+    @pl.when(me > 0)
+    def _():
+        pl.semaphore_wait(barrier, (level + 1) * (1 + side[0]) * (1 + side[1]) - 1 + core)
+
+    for d in range(plane):
+        def answer(d=d):
+            @pl.loop(0, level + (d != 0))
+            def _(z):
+                greet(flags.at[chip], device_of(z, around[d]))
+
+        answer() if d == 0 else pl.when(below[d])(answer)
+
+    def introduce(za, qa, zb, qb):
+        greet(flags.at[zb * plane + qb], device_of(za, qa))
+        greet(flags.at[za * plane + qa], device_of(zb, qb))
+
+    for q in range(1, plane):
+        @pl.when(here == q)
+        def _():
+            if q == plane - 1:
+                introduce(level, 1, level, 2)
+
+            @pl.loop(0, level)
+            def _(z):
+                for low_q in range(plane):
+                    for high_q in range(plane):
+                        if low_q | high_q == q and high_q != q:
+                            if low_q & ~high_q:
+                                introduce(z, low_q, level, high_q)
+
+    @pl.when(core == 1)
+    def _():
+        greet(partner_flag, partner)
+
+    for edge in (pl.ds(0, BELOW), pl.ds(BELOW + ny, ABOVE)):
+        rows_of_y[edge] = jnp.zeros((edge.size, pairs, lanes), jnp.float32)
     for p in range(pairs):
-        send[pl.ds(p, ny, stride=pairs), :] = points_ref[p].T
-    span_base = functools.partial(span_of, me, jl, ny)
-    make_weights(dims, me, span_base, oy_ref, cy_ref, oz_ref, cz_ref, cx_ref, wx_ref, wy, rz, rz_lo)
-    held[me, middle] = rows_of_y[pl.ds(chip * own, own)]
-
-    pl.semaphore_wait(barrier, n - 1)
+        loads[p].wait()
+        send[pl.ds(BELOW * pairs + p, ny, stride=pairs), :] = slab[p].T
 
     def remote(src, dst, send_sem, recv_sem, device):
         return pltpu.make_async_remote_copy(
@@ -240,180 +314,194 @@
             device_id=(device,), device_id_type=MESH,
         )
 
-    def main_copy(k):
-        target = flip(chip, k, chips)
+    def await_recv(ref, semaphore):
+        remote(ref, ref, out_sem, semaphore, partner).wait_recv()
+
+    def await_send(count, semaphore):
+        rows = any_rows.at[pl.ds(0, count)]
+        remote(rows, rows, semaphore, pass_recv.at[0], partner).wait_send()
+
+    def put(z, q, rows, semaphores):
+        remote(
+            rows_of_y.at[pl.ds((z * plane + q) * own + rows.start, rows.size)],
+            direct.at[level, here, rows], out_sem, semaphores.at[level],
+            (z * plane + q) * 2 + core,
+        ).start()
+
+    def ask(mine, z, d):
+        def wait():
+            pl.semaphore_wait(flags.at[z * plane + around[d]], 1)
+
+        if z > mine:
+            wait()
+        elif d:
+            pl.when(missing[d])(wait)
+
+    def send_whole(mine, targets):
+        for d in range(plane):
+            for z in targets:
+                ask(mine, z, d)
+                put(z, around[d], whole, whole_recv)
+
+    def send_ends(mine, targets):
+        for d in range(plane):
+            for z in targets:
+                ask(mine, z, d)
+                put(z, around[d], low, low_recv)
+
+                @pl.when(around[d] == plane - 1)
+                def _():
+                    put(z, around[d], high, high_recv)
+
+    def send_middle(mine, targets):
+        for d in range(plane)[::-1]:
+            for z in targets:
+                put(z, around[d], middle, middle_recv)
+
+    def send_plane(mine, targets):
+        for d in range(1, plane):
+            ask(mine, mine, d)
+            put(mine, around[d], whole, whole_recv)
+
+    def pass_copy(z):
         return remote(
-            rows_of_y.at[pl.ds(target * own, own)], held.at[me, middle],
-            main_send.at[k], main_recv.at[k], target * 2 + core,
-        )
-
-    def main_arrival(k):
-        source = flip(chip, k, chips) * 2 + core
-        return remote(held.at[source, middle], held.at[source, middle], main_send.at[k], main_recv.at[k], partner)
-
-    def pass_copy(k):
-        source = flip(chip, k, chips) * 2 + core
-        return remote(held.at[source, middle], held.at[source, middle], pass_send.at[k], pass_recv.at[k], partner)
-
-    def pass_arrival(k):
-        source = flip(chip, k, chips) * 2 + 1 - core
-        return remote(held.at[source, middle], held.at[source, middle], pass_send.at[k], pass_recv.at[k], partner)
-
-    def up_copy(k):
-        source = flip(chip, k, chips) * 2 + core
-        return remote(
-            held.at[source, pl.ds(own, BELOW)], held.at[source, pl.ds(0, BELOW)],
-            up_send.at[k], halo_recv.at[source], chip * 2 + 2,
-        )
-
-    def down_copy(k):
-        source = flip(chip, k, chips) * 2 + core
-        return remote(
-            held.at[source, pl.ds(BELOW, ABOVE)], held.at[source, pl.ds(BELOW + own, ABOVE)],
-            down_send.at[k], halo_recv.at[source], chip * 2 - 1,
-        )
-
-    has_up = here < plane - 1
-    has_down = here > 0
-
-    def edge_below(g):
-        target = flip(level, g, PLANES) * plane
-        copy = lambda: remote(
-            rows_of_y.at[pl.ds(target * own - BELOW, BELOW)], held.at[me, pl.ds(0, BELOW)],
-            edge_send.at[g], halo_recv.at[me], target * 2,
-        )
-        return (target > 0) & (target * 2 != me), copy
-
-    def edge_above(g):
-        target = flip(level, g, PLANES) * plane + plane - 1
-        copy = lambda: remote(
-            rows_of_y.at[pl.ds(target * own + own, ABOVE)], held.at[me, pl.ds(BELOW + own, ABOVE)],
-            edge_send.at[PLANES + g], halo_recv.at[me], target * 2 + 1,
-        )
-        return (target < chips - 1) & (target * 2 + 1 != me), copy
-
-    def send_edges(g):
-        for edge in (edge_below, edge_above):
-            needed, copy = edge(g)
-
-            @pl.when(needed)
-            def _():
-                copy().start()
-
-    def hand_on(k):
-        pass_copy(k).start()
-
-        @pl.when(has_up)
-        def _():
-            up_copy(k).start()
-
-        @pl.when(has_down)
-        def _():
-            down_copy(k).start()
-
-    @pl.loop(1, plane)
-    def _(k):
-        main_copy(k).start()
-
-    send_edges(0)
-    hand_on(0)
-
-    for g in range(1, PLANES):
-
-        @pl.loop(g * plane, (g + 1) * plane)
-        def _(k):
-            main_copy(k).start()
-
-        send_edges(g)
-
-    at_bottom = (here == 0) & (core == 0)
-    at_top = (here == plane - 1) & (core == 1)
-
-    @pl.when(at_bottom & (chip > 0))
-    def _():
-        held[me, 0:BELOW] = rows_of_y[pl.ds(chip * own - BELOW, BELOW)]
-
-    @pl.when(at_top & (chip < chips - 1))
-    def _():
-        held[me, BELOW + own :] = rows_of_y[pl.ds(chip * own + own, ABOVE)]
-
-    def await_halo(source):
-        away = (source != me) | ((here != 0) & (core == 0)) | ((here != plane - 1) & (core == 1))
-
-        @pl.when(away & (core == 0) & (chip > 0))
-        def _():
-            rows = held.at[source, pl.ds(0, BELOW)]
-            remote(rows, rows, up_send.at[0], halo_recv.at[source], partner).wait_recv()
-
-        @pl.when(away & (core == 1) & (chip < chips - 1))
-        def _():
-            rows = held.at[source, pl.ds(BELOW + own, ABOVE)]
-            remote(rows, rows, up_send.at[0], halo_recv.at[source], partner).wait_recv()
-
-    def refine(k):
-        others = [flip(chip, k + i, chips) * 2 for i in range(2)]
-        for i in range(2):
-            pass_arrival(k + i).wait_recv()
-        devices = [other + c for other in others for c in range(2)]
-        for device in devices:
-            await_halo(device)
+            direct.at[z, :, pl.ds((1 - core) * half, narrow)], passed.at[z],
+            pass_sem, pass_recv.at[z], partner,
+        )
+
+    def refine(blocks, base, devices):
         for j in range(jl):
-            row = span_base(j) - (chip * own - BELOW)
-            sums = [None] * len(devices)
+            row = span_base(j) - base
+            sums = [None] * len(blocks)
             for m in range(SPAN):
                 weight = wy[j * SPAN + m]
-                for i, device in enumerate(devices):
-                    term = weight * held[device, row + m]
+                for i, block in enumerate(blocks):
+                    term = weight * block[row + m]
                     sums[i] = term if m == 0 else sums[i] + term
             for i, total in enumerate(sums):
                 mixed[pl.ds(i * pairs * jl + j, pairs, stride=jl), :] = total
         refine_z(dims, pairs, mixed, rz, rz_lo, grid_ref, devices)
 
-    def take(k):
-        main_arrival(k).wait_recv()
-        hand_on(k)
-
-    @pl.loop(1, plane)
-    def _(k):
-        take(k)
-
-    @pl.loop(1, PLANES)
-    def _(g):
-        @pl.loop(0, plane)
-        def _(r):
-            take(g * plane + r)
-
-        @pl.loop(0, plane // 2)
-        def _(h):
-            refine((g - 1) * plane + 2 * h)
-
-    @pl.loop((chips - plane) // 2, chips // 2)
-    def _(h):
-        refine(2 * h)
-
-    @pl.loop(1, chips)
-    def _(k):
-        main_copy(k).wait_send()
-
-    @pl.loop(0, chips)
-    def _(k):
-        pass_copy(k).wait_send()
-
-        @pl.when(has_up)
+    def take_whole(z):
+        await_recv(direct.at[z], whole_recv.at[z])
+        pass_copy(z).start()
+
+    def take_plane(z):
+        await_recv(direct.at[z, pl.ds(0, plane - 1)], whole_recv.at[z])
+        pass_copy(z).start()
+
+    def take_low(z):
+        await_recv(direct.at[z, :, low], low_recv.at[z])
+
+        @pl.when(here > 0)
         def _():
-            up_copy(k).wait_send()
-
-        @pl.when(has_down)
+            remote(
+                direct.at[z, :, low], direct.at[z, :, high], hand_sem, high_recv.at[z], (chip - 1) * 2 + core
+            ).start()
+
+    def take_middle(z):
+        await_recv(direct.at[z, :, high], high_recv.at[z])
+        await_recv(direct.at[z, :, middle], middle_recv.at[z])
+        pass_copy(z).start()
+
+    def near(z):
+        refine(
+            [direct.at[z, q] for q in range(plane)], chip * own - BELOW,
+            [(z * plane + q) * 2 + core for q in range(plane)],
+        )
+
+    def far(z):
+        pass_copy(z).wait_recv()
+        refine(
+            [passed.at[z, q] for q in range(plane)], me * half - BELOW,
+            [(z * plane + q) * 2 + 1 - core for q in range(plane)],
+        )
+
+    mx = wx_ref.shape[1]
+    part, margin = mx // PLANES, GROUP
+
+    def across(*zs):
+        first, last = min(zs), max(zs) + 1
+        start = first * part
+        stop = last * part
+        if len(zs) > 1:
+            start += margin * (first > 0)
+            stop -= margin * (last < PLANES)
+        elif first in (0, PLANES - 1):
+            start += margin * (first > 0)
+            stop -= margin * (last < PLANES)
+        else:
+            start -= margin
+            stop += margin
+        refine_rows(start, stop)
+
+    def refine_rows(start, stop):
+        @pl.loop(start // GROUP, stop // GROUP)
+        def _(g):
+            done = []
+            for r in range(GROUP):
+                i = g * GROUP + r
+                first = ox_ref[i]
+                weights = [wx_scalars[k, i] for k in range(BAND)]
+                for c in range(comps):
+                    acc = weights[0] * grid_ref[c, first]
+                    for k in range(1, BAND):
+                        acc = acc + weights[k] * grid_ref[c, first + k]
+                    done.append((c, i, acc))
+            for c, i, acc in done:
+                block_ref[c, i] = acc
+
+    acts = {
+        "W": send_whole, "E": send_ends, "M": send_middle, "P": send_plane,
+        "w": take_whole, "p": take_plane, "e": take_low, "m": take_middle, "n": near, "f": far, "x": across,
+    }
+    sends = [
+        ["P0", "W1", "E2", "E3", "M2", "M3"],
+        ["W0", "P1", "E2", "E3", "M2", "M3"],
+        ["E01", "P2", "W3", "M0", "M1"],
+        ["E01", "W2", "P3", "M0", "M1"],
+    ]
+    takes = [
+        ["p0", "n0", "e3", "e2", "f0", "w1", "n1", "f1", "x01", "m3", "n3", "f3", "x3", "m2", "n2", "f2", "x2"],
+        ["p1", "n1", "w0", "n0", "f1", "e3", "e2", "f0", "x01", "m3", "n3", "f3", "x3", "m2", "n2", "f2", "x2"],
+        ["p2", "n2", "e1", "e0", "f2", "w3", "n3", "f3", "x23", "m0", "n0", "f0", "x0", "m1", "n1", "f1", "x1"],
+        ["p3", "n3", "w2", "n2", "f3", "e0", "e1", "f2", "x23", "m0", "n0", "f0", "x0", "m1", "n1", "f1", "x1"],
+    ]
+
+    for z, plan in enumerate(sends):
+
+        @pl.when(level == z)
         def _():
-            down_copy(k).wait_send()
-
-    for g in range(PLANES):
-        for edge in (edge_below, edge_above):
-            needed, copy = edge(g)
-
-            @pl.when(needed)
-            def _():
-                copy().wait_send()
+            for step in plan:
+                acts[step[0]](z, [int(target) for target in step[1:]])
+
+    direct[level, here] = rows_of_y[pl.ds(chip * own, wide)]
+
+    @pl.when(core == 0)
+    def _():
+        pl.semaphore_wait(partner_flag, 1)
+
+    for small in smalls:
+        small.wait()
+    make_weights(dims, me, span_base, oy_ref, cy_ref, oz_ref, cz_ref, cx_ref, wx_ref, wy, rz, rz_lo)
+    scalars = pltpu.make_async_copy(wx_ref, wx_scalars, small_sem.at[0])
+    scalars.start()
+    scalars.wait()
+
+    for z, plan in enumerate(takes):
+
+        @pl.when(level == z)
+        def _():
+            for step in plan:
+                acts[step[0]](*[int(target) for target in step[1:]])
+
+    await_send(2 * (plane * own + REACH) + (2 * plane - 1) * wide, out_sem)
+
+    @pl.when(here > 0)
+    def _():
+        await_send(2 * plane * REACH, hand_sem)
+
+    await_send(PLANES * plane * narrow, pass_sem)
 
 
 def refine_x(steps, ox_ref, wx_ref, grid_ref, out_ref, block, sems):
@@ -448,6 +536,14 @@
         put(s).wait()
 
 
+def store(block_ref, out_ref, sems):
+    copies = [pltpu.make_async_copy(block_ref.at[c], out_ref.at[c], sems.at[c]) for c in range(block_ref.shape[0])]
+    for copy in copies:
+        copy.start()
+    for copy in copies:
+        copy.wait()
+
+
 def solution(mesh):
     n = mesh.shape["slab"]
     vmem = pl.BlockSpec(memory_space=pltpu.VMEM)
@@ -466,19 +562,61 @@
         wide, narrow = 2 * cl + REACH, cl + REACH
         slab = jnp.transpose(points, (0, 1, 3, 2)).reshape(pairs, lanes, ny)
         f32, bf16 = jnp.float32, jnp.bfloat16
-        if jl >= ABOVE and chips % PLANES == 0:
-            kernel, name = relay, "relay"
-            buffers = [pltpu.VMEM((n, BELOW + jl + ABOVE, pairs, lanes), f32)]
-            counts = [chips] * 6 + [n, 2 * PLANES]
-        else:
-            kernel, name = exchange, "exchange"
-            buffers = [
-                pltpu.VMEM((chips, wide, pairs, lanes), f32),
-                pltpu.VMEM((chips, narrow, pairs, lanes), f32),
-            ]
-            counts = [chips] * 4
+        f32_rows = lambda *shape: pltpu.VMEM((*shape, pairs, lanes), f32)
+        shared = [
+            pltpu.VMEM((jl * SPAN, pairs, lanes), f32),
+            pltpu.VMEM((2 * lanes, fold * mz), bf16),
+            pltpu.VMEM((lanes, fold * mz), bf16),
+            pltpu.VMEM((4 * pairs * jl, lanes), f32),
+        ]
+        semaphores = lambda *shape: pltpu.SemaphoreType.DMA(shape)
+        if jl > REACH and chips == PLANES * PLANES and my == 2 * ny and mx % (PLANES * GROUP) == 0:
+            plane = chips // PLANES
+            limit = VMEM_MOST - 4 * comps * mx * jl * mz
+            hbm = pl.BlockSpec(memory_space=pltpu.HBM)
+            block = pl.pallas_call(
+                functools.partial(relay, (n, comps, xl, ny, nz, jl, mz)),
+                out_shape=pltpu.VMEM((comps, mx, jl, mz), f32),
+                in_specs=[hbm] * 7,
+                out_specs=vmem,
+                scratch_shapes=[
+                    pltpu.VMEM((pairs, lanes, ny), f32),
+                    pltpu.VMEM(((ny + REACH) * pairs, lanes), f32),
+                    f32_rows(PLANES, plane, jl + REACH),
+                    f32_rows(PLANES, plane, cl + REACH),
+                    *shared,
+                    pltpu.SMEM((my,), jnp.int32),
+                    pltpu.SMEM((BAND, my), f32),
+                    pltpu.VMEM((1, mz), jnp.int32),
+                    pltpu.VMEM((BAND, mz), f32),
+                    pltpu.VMEM((BAND, mx), f32),
+                    pltpu.VMEM((comps, nx, jl, mz), f32),
+                    pltpu.SMEM((mx,), jnp.int32),
+                    pltpu.VMEM((BAND, mx), f32),
+                    pltpu.SMEM((BAND, mx), f32),
+                    semaphores(pairs),
+                    semaphores(6),
+                    *[pltpu.SemaphoreType.DMA] * 3,
+                    *[semaphores(PLANES)] * 5,
+                    pltpu.SemaphoreType.REGULAR((chips,)),
+                    pltpu.SemaphoreType.REGULAR,
+                ],
+                compiler_params=pltpu.CompilerParams(
+                    collective_id=0, has_side_effects=True, vmem_limit_bytes=limit
+                ),
+                name="relay",
+            )(slab, offsets_y, coeffs_y, offsets_z.reshape(1, mz), coeffs_z, coeffs_x, offsets_x)
+            return pl.pallas_call(
+                store,
+                out_shape=jax.ShapeDtypeStruct((comps, mx, jl, mz), f32),
+                in_specs=[vmem],
+                out_specs=pl.BlockSpec(memory_space=pltpu.HBM),
+                scratch_shapes=[semaphores(comps)],
+                compiler_params=pltpu.CompilerParams(vmem_limit_bytes=limit),
+                name="store",
+            )(pltpu.with_memory_space_constraint(block, pltpu.VMEM))
         grid, wx = pl.pallas_call(
-            functools.partial(kernel, (n, comps, xl, ny, nz, jl, mz)),
+            functools.partial(exchange, (n, comps, xl, ny, nz, jl, mz)),
             out_shape=(
                 pltpu.VMEM((comps, nx, jl, mz), f32),
                 jax.ShapeDtypeStruct((BAND, mx), f32),
@@ -487,15 +625,13 @@
             out_specs=(vmem, vmem),
             scratch_shapes=[
                 pltpu.VMEM((ny * pairs, lanes), f32),
-                *buffers,
-                pltpu.VMEM((jl * SPAN, pairs, lanes), f32),
-                pltpu.VMEM((2 * lanes, fold * mz), bf16),
-                pltpu.VMEM((lanes, fold * mz), bf16),
-                pltpu.VMEM((4 * pairs * jl, lanes), f32),
-                *[pltpu.SemaphoreType.DMA((count,)) for count in counts],
+                f32_rows(chips, wide),
+                f32_rows(chips, narrow),
+                *shared,
+                *[semaphores(chips)] * 4,
             ],
             compiler_params=pltpu.CompilerParams(collective_id=0, has_side_effects=True),
-            name=name,
+            name="exchange",
         )(slab, offsets_y, coeffs_y, offsets_z.reshape(1, mz), coeffs_z, coeffs_x)
         steps = 8
         return pl.pallas_call(

time: 29.2 us -> 26.1 us (0.89)
  the two profiles are of different devices: /device:TPU:11 before, /device:TPU:1 now
where the time goes in v1:
time: 26.1 us; the launch traced here: 25.9 us
  Pallas kernels  25.9 us (99%)
    pallas_call x1, Pallas kernels, body(): pl.pallas_call(functools.partial(relay, (n, comps, xl, ny, nz, jl, mz)),...  23.8 us
    pallas_call x1, Pallas kernels, body(): pl.pallas_call(store, out_shape=jax.ShapeDtypeStruct((comps, mx, jl, mz),...  2.04 us

profile of v1, /device:TPU:1, one launch (start us, length us, event | category | flops | bytes accessed | tf_op | source)
XLA Modules:
  0.0 25.9 jit_solution(15596685649104527123)
XLA Ops:
  0.0 23.8 %relay.1.block_ref = f32[4,256,8,128]{3,2,1,0:T(8,128)S(1)} custom-call(f32[8,128,128]{2,1,0:T(8,128)} %bitcast.4, s32[256]{0:T(256)} %oy_hbm.1, f32[4,256]{1,0:T(4,128)} %cy_hbm.1, s32[1,128]{1,0:T(1,128)} %bitcast.5, f32[4,128]{1,0:T(4,128)} %cz_hbm.1, f32[4,256]{1,0:T(4,128)} %cx_hbm.1, s32[256]{0:T(256)} %ox_hbm.1), custom_call_target="tpu_custom_call" | custom-call | tf_op jit(solution)/shard_map/relay/pallas_call | solution.py:577
  23.9 2.0 %store.1 = f32[4,256,8,128]{3,2,1,0:T(8,128)} custom-call(f32[4,256,8,128]{3,2,1,0:T(8,128)S(1)} %relay.1.block_ref), custom_call_target="tpu_custom_call" | custom-call | tf_op jit(solution)/shard_map/store/pallas_call | solution.py:609

commit v2 on v1

--- a/solution.py
+++ b/solution.py
@@ -221,6 +221,7 @@
     wide, narrow = own + REACH, half + REACH
     whole, low, high = pl.ds(0, wide), pl.ds(0, REACH), pl.ds(own, REACH)
     middle = pl.ds(REACH, own - REACH)
+    low_inside, high_inside = pl.ds(BELOW, ABOVE), pl.ds(own, BELOW)
     me = lax.axis_index("slab")
     chip, core = lax.div(me, 2), lax.rem(me, 2)
     partner = chip * 2 + 1 - core
@@ -304,8 +305,9 @@
 
     for edge in (pl.ds(0, BELOW), pl.ds(BELOW + ny, ABOVE)):
         rows_of_y[edge] = jnp.zeros((edge.size, pairs, lanes), jnp.float32)
+    for load in loads:
+        load.wait()
     for p in range(pairs):
-        loads[p].wait()
         send[pl.ds(BELOW * pairs + p, ny, stride=pairs), :] = slab[p].T
 
     def remote(src, dst, send_sem, recv_sem, device):
@@ -328,40 +330,41 @@
             (z * plane + q) * 2 + core,
         ).start()
 
-    def ask(mine, z, d):
+    lacking = [None, side[0] == 0, side[1] == 0, here < plane - 1]
+
+    def pick(mine, z, i):
+        if z < mine:
+            q, unknown = i, lacking[i]
+        else:
+            q, unknown = around[i], True if z > mine else missing[i]
+
         def wait():
-            pl.semaphore_wait(flags.at[z * plane + around[d]], 1)
-
-        if z > mine:
+            pl.semaphore_wait(flags.at[z * plane + q], 1)
+
+        if unknown is True:
             wait()
-        elif d:
-            pl.when(missing[d])(wait)
-
-    def send_whole(mine, targets):
-        for d in range(plane):
-            for z in targets:
-                ask(mine, z, d)
-                put(z, around[d], whole, whole_recv)
-
-    def send_ends(mine, targets):
-        for d in range(plane):
-            for z in targets:
-                ask(mine, z, d)
-                put(z, around[d], low, low_recv)
-
-                @pl.when(around[d] == plane - 1)
-                def _():
-                    put(z, around[d], high, high_recv)
-
-    def send_middle(mine, targets):
-        for d in range(plane)[::-1]:
-            for z in targets:
-                put(z, around[d], middle, middle_recv)
-
-    def send_plane(mine, targets):
-        for d in range(1, plane):
-            ask(mine, mine, d)
-            put(mine, around[d], whole, whole_recv)
+        elif unknown is not None:
+            pl.when(unknown)(wait)
+        return q
+
+    def send_whole(mine, z, places):
+        for i in places:
+            put(z, pick(mine, z, i), whole, whole_recv)
+
+    def send_ends(mine, z, places):
+        for i in places:
+            q = pick(mine, z, i)
+            if z == 0:
+                pl.when(q == 0)(functools.partial(put, z, q, low_inside, low_recv))
+                pl.when(q > 0)(functools.partial(put, z, q, low, low_recv))
+            else:
+                put(z, q, low, low_recv)
+            edge = high_inside if z == PLANES - 1 else high
+            pl.when(q == plane - 1)(functools.partial(put, z, q, edge, high_recv))
+
+    def send_middle(mine, z, places):
+        for i in places if z < mine else places[::-1]:
+            put(z, i if z < mine else around[i], middle, middle_recv)
 
     def pass_copy(z):
         return remote(
@@ -391,7 +394,13 @@
         pass_copy(z).start()
 
     def take_low(z):
-        await_recv(direct.at[z, :, low], low_recv.at[z])
+        @pl.when(chip > 0)
+        def _():
+            await_recv(direct.at[z, :, low], low_recv.at[z])
+
+        @pl.when(chip == 0)
+        def _():
+            await_recv(direct.at[z, :, low_inside], low_recv.at[z])
 
         @pl.when(here > 0)
         def _():
@@ -400,7 +409,14 @@
             ).start()
 
     def take_middle(z):
-        await_recv(direct.at[z, :, high], high_recv.at[z])
+        @pl.when(chip < chips - 1)
+        def _():
+            await_recv(direct.at[z, :, high], high_recv.at[z])
+
+        @pl.when(chip == chips - 1)
+        def _():
+            await_recv(direct.at[z, :, high_inside], high_recv.at[z])
+
         await_recv(direct.at[z, :, middle], middle_recv.at[z])
         pass_copy(z).start()
 
@@ -417,26 +433,26 @@
             [(z * plane + q) * 2 + 1 - core for q in range(plane)],
         )
 
-    mx = wx_ref.shape[1]
-    part, margin = mx // PLANES, GROUP
-
-    def across(*zs):
-        first, last = min(zs), max(zs) + 1
-        start = first * part
-        stop = last * part
-        if len(zs) > 1:
-            start += margin * (first > 0)
-            stop -= margin * (last < PLANES)
-        elif first in (0, PLANES - 1):
-            start += margin * (first > 0)
-            stop -= margin * (last < PLANES)
-        else:
-            start -= margin
-            stop += margin
-        refine_rows(start, stop)
+    mx, nx = wx_ref.shape[1], n * xl
+    depth = nx // PLANES
+
+    def across(known, written):
+        fresh = []
+        for g in range(mx // GROUP):
+            low_x = max(g * GROUP // 2 - BELOW, 0)
+            high_x = min((g * GROUP + GROUP - 1) // 2 + ABOVE, nx - 1)
+            if g not in written and set(range(low_x // depth, high_x // depth + 1)) <= known:
+                fresh.append(g)
+        written.update(fresh)
+        starts = [g for g in fresh if g - 1 not in fresh]
+        for start in starts:
+            stop = start
+            while stop in fresh:
+                stop += 1
+            refine_rows(start, stop)
 
     def refine_rows(start, stop):
-        @pl.loop(start // GROUP, stop // GROUP)
+        @pl.loop(start, stop)
         def _(g):
             done = []
             for r in range(GROUP):
@@ -452,20 +468,20 @@
                 block_ref[c, i] = acc
 
     acts = {
-        "W": send_whole, "E": send_ends, "M": send_middle, "P": send_plane,
-        "w": take_whole, "p": take_plane, "e": take_low, "m": take_middle, "n": near, "f": far, "x": across,
+        "W": send_whole, "E": send_ends, "M": send_middle,
+        "w": take_whole, "p": take_plane, "e": take_low, "m": take_middle, "n": near, "f": far,
     }
     sends = [
-        ["P0", "W1", "E2", "E3", "M2", "M3"],
-        ["W0", "P1", "E2", "E3", "M2", "M3"],
-        ["E01", "P2", "W3", "M0", "M1"],
-        ["E01", "W2", "P3", "M0", "M1"],
+        ["W0:123", "W1", "E2", "E3", "M3", "M2"],
+        ["W0", "W1:123", "E2", "E3", "M3", "M2"],
+        ["E0:012", "E1:012", "E0:3", "E1:3", "W2:123", "W3", "M0", "M1"],
+        ["E0:012", "E1:012", "E0:3", "E1:3", "W2", "W3:123", "M0", "M1"],
     ]
     takes = [
-        ["p0", "n0", "e3", "e2", "f0", "w1", "n1", "f1", "x01", "m3", "n3", "f3", "x3", "m2", "n2", "f2", "x2"],
-        ["p1", "n1", "w0", "n0", "f1", "e3", "e2", "f0", "x01", "m3", "n3", "f3", "x3", "m2", "n2", "f2", "x2"],
-        ["p2", "n2", "e1", "e0", "f2", "w3", "n3", "f3", "x23", "m0", "n0", "f0", "x0", "m1", "n1", "f1", "x1"],
-        ["p3", "n3", "w2", "n2", "f3", "e0", "e1", "f2", "x23", "m0", "n0", "f0", "x0", "m1", "n1", "f1", "x1"],
+        ["p0", "n0", "e2", "f0", "w1", "n1", "e3", "f1", "x", "m2", "n2", "m3", "f2", "x", "n3", "f3", "x"],
+        ["p1", "n1", "w0", "n0", "f1", "e3", "f0", "x", "e2", "m3", "n3", "m2", "f3", "n2", "x", "f2", "x"],
+        ["p2", "n2", "e1", "f2", "e0", "w3", "n3", "f3", "x", "m0", "n0", "m1", "f0", "n1", "x", "f1", "x"],
+        ["p3", "n3", "w2", "n2", "f3", "e0", "f2", "x", "e1", "m0", "n0", "m1", "f0", "n1", "x", "f1", "x"],
     ]
 
     for z, plan in enumerate(sends):
@@ -473,7 +489,8 @@
         @pl.when(level == z)
         def _():
             for step in plan:
-                acts[step[0]](z, [int(target) for target in step[1:]])
+                target, _, places = step[1:].partition(":")
+                acts[step[0]](z, int(target), [int(i) for i in places] or list(range(plane)))
 
     direct[level, here] = rows_of_y[pl.ds(chip * own, wide)]
 
@@ -492,10 +509,24 @@
 
         @pl.when(level == z)
         def _():
+            known, written = set(), set()
             for step in plan:
-                acts[step[0]](*[int(target) for target in step[1:]])
-
-    await_send(2 * (plane * own + REACH) + (2 * plane - 1) * wide, out_sem)
+                if step == "x":
+                    across(known, written)
+                else:
+                    acts[step[0]](int(step[1]))
+                    known |= {int(step[1])} if step[0] == "f" else set()
+            assert len(written) == mx // GROUP
+
+    ends = 2 * (plane * own + REACH) + (2 * plane - 1) * wide
+
+    @pl.when(lax.div(level, 2) == 0)
+    def _():
+        await_send(ends - ABOVE, out_sem)
+
+    @pl.when(lax.div(level, 2) == 1)
+    def _():
+        await_send(ends - BELOW, out_sem)
 
     @pl.when(here > 0)
     def _():

time: 26.1 us -> 24.7 us (0.946)
  the two profiles are of different devices: /device:TPU:1 before, /device:TPU:25 now
where the time goes in v2:
time: 24.7 us; the launch traced here: 24.5 us
  Pallas kernels  24.5 us (99%)
    pallas_call x1, Pallas kernels, body(): pl.pallas_call(functools.partial(relay, (n, comps, xl, ny, nz, jl, mz)),...  22.5 us
    pallas_call x1, Pallas kernels, body(): pl.pallas_call(store, out_shape=jax.ShapeDtypeStruct((comps, mx, jl, mz),...  2.04 us

profile of v2, /device:TPU:25, one launch (start us, length us, event | category | flops | bytes accessed | tf_op | source)
XLA Modules:
  0.0 24.5 jit_solution(3984702268725441336)
XLA Ops:
  0.0 22.5 %relay.1.block_ref = f32[4,256,8,128]{3,2,1,0:T(8,128)S(1)} custom-call(f32[8,128,128]{2,1,0:T(8,128)} %bitcast.4, s32[256]{0:T(256)} %oy_hbm.1, f32[4,256]{1,0:T(4,128)} %cy_hbm.1, s32[1,128]{1,0:T(1,128)} %bitcast.5, f32[4,128]{1,0:T(4,128)} %cz_hbm.1, f32[4,256]{1,0:T(4,128)} %cx_hbm.1, s32[256]{0:T(256)} %ox_hbm.1), custom_call_target="tpu_custom_call" | custom-call | tf_op jit(solution)/shard_map/relay/pallas_call | solution.py:608
  22.5 2.0 %store.1 = f32[4,256,8,128]{3,2,1,0:T(8,128)} custom-call(f32[4,256,8,128]{3,2,1,0:T(8,128)S(1)} %relay.1.block_ref), custom_call_target="tpu_custom_call" | custom-call | tf_op jit(solution)/shard_map/store/pallas_call | solution.py:640

commit v3 on v2

--- a/solution.py
+++ b/solution.py
@@ -15,6 +15,7 @@
 PLANES = 4
 GROUP = 8
 VMEM_MOST = 67043328
+LAST = (3, 2, 1, 1)
 
 
 def flip(a, k, chips):
@@ -205,10 +206,10 @@
 def relay(
     dims,
     points_hbm, oy_hbm, cy_hbm, oz_hbm, cz_hbm, cx_hbm, ox_hbm,
-    block_ref,
+    block_ref, grid_ref, wx_ref,
     slab, send, direct, passed, wy, rz, rz_lo, mixed,
     oy_ref, cy_ref, oz_ref, cz_ref, cx_ref,
-    grid_ref, ox_ref, wx_ref, wx_scalars,
+    ox_ref, wx_scalars,
     load_sem, small_sem, out_sem, hand_sem, pass_sem,
     whole_recv, low_recv, high_recv, middle_recv, pass_recv,
     flags, partner_flag,
@@ -434,54 +435,28 @@
         )
 
     mx, nx = wx_ref.shape[1], n * xl
-    depth = nx // PLANES
 
     def across(known, written):
-        fresh = []
-        for g in range(mx // GROUP):
-            low_x = max(g * GROUP // 2 - BELOW, 0)
-            high_x = min((g * GROUP + GROUP - 1) // 2 + ABOVE, nx - 1)
-            if g not in written and set(range(low_x // depth, high_x // depth + 1)) <= known:
-                fresh.append(g)
-        written.update(fresh)
-        starts = [g for g in fresh if g - 1 not in fresh]
-        for start in starts:
-            stop = start
-            while stop in fresh:
-                stop += 1
-            refine_rows(start, stop)
-
-    def refine_rows(start, stop):
-        @pl.loop(start, stop)
-        def _(g):
-            done = []
-            for r in range(GROUP):
-                i = g * GROUP + r
-                first = ox_ref[i]
-                weights = [wx_scalars[k, i] for k in range(BAND)]
-                for c in range(comps):
-                    acc = weights[0] * grid_ref[c, first]
-                    for k in range(1, BAND):
-                        acc = acc + weights[k] * grid_ref[c, first + k]
-                    done.append((c, i, acc))
-            for c, i, acc in done:
-                block_ref[c, i] = acc
+        fresh = groups_in(known, mx, nx) - written
+        written |= fresh
+        for start, stop in runs(fresh):
+            refine_rows(start, stop, ox_ref, wx_scalars, grid_ref, block_ref)
 
     acts = {
         "W": send_whole, "E": send_ends, "M": send_middle,
         "w": take_whole, "p": take_plane, "e": take_low, "m": take_middle, "n": near, "f": far,
     }
     sends = [
-        ["W0:123", "W1", "E2", "E3", "M3", "M2"],
+        ["W1:0", "W0:123", "E2", "E3", "W1:123", "M3", "M2"],
         ["W0", "W1:123", "E2", "E3", "M3", "M2"],
-        ["E0:012", "E1:012", "E0:3", "E1:3", "W2:123", "W3", "M0", "M1"],
+        ["W3:0", "E0:012", "E1:012", "W3:12", "E0:3", "E1:3", "W3:3", "W2:123", "M0", "M1"],
         ["E0:012", "E1:012", "E0:3", "E1:3", "W2", "W3:123", "M0", "M1"],
     ]
     takes = [
-        ["p0", "n0", "e2", "f0", "w1", "n1", "e3", "f1", "x", "m2", "n2", "m3", "f2", "x", "n3", "f3", "x"],
-        ["p1", "n1", "w0", "n0", "f1", "e3", "f0", "x", "e2", "m3", "n3", "m2", "f3", "n2", "x", "f2", "x"],
-        ["p2", "n2", "e1", "f2", "e0", "w3", "n3", "f3", "x", "m0", "n0", "m1", "f0", "n1", "x", "f1", "x"],
-        ["p3", "n3", "w2", "n2", "f3", "e0", "f2", "x", "e1", "m0", "n0", "m1", "f0", "n1", "x", "f1", "x"],
+        ["p0", "n0", "e2", "f0", "w1", "n1", "e3", "f1", "x", "m2", "n2", "m3", "f2", "x", "n3", "f3"],
+        ["p1", "n1", "e3", "f1", "w0", "n0", "e2", "f0", "x", "m3", "n3", "m2", "f3", "n2", "x", "f2"],
+        ["p2", "n2", "e1", "f2", "e0", "w3", "n3", "f3", "x", "m0", "n0", "m1", "f0", "n1", "x", "f1"],
+        ["p3", "n3", "w2", "n2", "f3", "e0", "f2", "x", "e1", "m0", "n0", "m1", "f0", "n1", "x", "f1"],
     ]
 
     for z, plan in enumerate(sends):
@@ -516,7 +491,7 @@
                 else:
                     acts[step[0]](int(step[1]))
                     known |= {int(step[1])} if step[0] == "f" else set()
-            assert len(written) == mx // GROUP
+            assert written == groups_in(set(range(PLANES)) - {LAST[z]}, mx, nx)
 
     ends = 2 * (plane * own + REACH) + (2 * plane - 1) * wide
 
@@ -567,12 +542,84 @@
         put(s).wait()
 
 
-def store(block_ref, out_ref, sems):
-    copies = [pltpu.make_async_copy(block_ref.at[c], out_ref.at[c], sems.at[c]) for c in range(block_ref.shape[0])]
-    for copy in copies:
-        copy.start()
-    for copy in copies:
-        copy.wait()
+def groups_in(known, mx, nx):
+    depth = nx // PLANES
+    inside = set()
+    for g in range(mx // GROUP):
+        low = max(g * GROUP // 2 - BELOW, 0) // depth
+        high = min((g * GROUP + GROUP - 1) // 2 + ABOVE, nx - 1) // depth
+        if set(range(low, high + 1)) <= known:
+            inside.add(g)
+    return inside
+
+
+def runs(groups):
+    out = []
+    for start in sorted(g for g in groups if g - 1 not in groups):
+        stop = start
+        while stop in groups:
+            stop += 1
+        out.append((start, stop))
+    return out
+
+
+def refine_rows(start, stop, ox_ref, wx_ref, grid_ref, block_ref):
+    comps = block_ref.shape[0]
+
+    @pl.loop(start, stop)
+    def _(g):
+        done = []
+        for r in range(GROUP):
+            i = g * GROUP + r
+            first = ox_ref[i]
+            weights = [wx_ref[k, i] for k in range(BAND)]
+            for c in range(comps):
+                acc = weights[0] * grid_ref[c, first]
+                for k in range(1, BAND):
+                    acc = acc + weights[k] * grid_ref[c, first + k]
+                done.append((c, i, acc))
+        for c, i, acc in done:
+            block_ref[c, i] = acc
+
+
+def finish(ready_ref, grid_ref, wx_hbm, ox_hbm, out_ref, late_ref, ox_ref, wx_ref, out_sem, late_sem, small_sem):
+    comps, mx = ready_ref.shape[:2]
+    nx = grid_ref.shape[1]
+    level = lax.div(lax.axis_index("slab"), 2 * PLANES)
+    smalls = [
+        pltpu.make_async_copy(src, dst, small_sem.at[i])
+        for i, (src, dst) in enumerate([(ox_hbm, ox_ref), (wx_hbm, wx_ref)])
+    ]
+    for small in smalls:
+        small.start()
+
+    def put(src, c, start, stop, sem):
+        rows = pl.ds(start * GROUP, (stop - start) * GROUP)
+        return pltpu.make_async_copy(src.at[c, rows], out_ref.at[c, rows], sem)
+
+    for z in range(PLANES):
+
+        @pl.when(level == z)
+        def _():
+            ready = groups_in(set(range(PLANES)) - {LAST[z]}, mx, nx)
+            late = runs(set(range(mx // GROUP)) - ready)
+            early = [
+                put(ready_ref, c, start, stop, out_sem.at[c, i])
+                for i, (start, stop) in enumerate(runs(ready))
+                for c in range(comps)
+            ]
+            for copy in early:
+                copy.start()
+            for small in smalls:
+                small.wait()
+            rest = []
+            for i, (start, stop) in enumerate(late):
+                refine_rows(start, stop, ox_ref, wx_ref, grid_ref, late_ref)
+                rest += [put(late_ref, c, start, stop, late_sem.at[c, i]) for c in range(comps)]
+            for copy in rest:
+                copy.start()
+            for copy in early + rest:
+                copy.wait()
 
 
 def solution(mesh):
@@ -603,13 +650,17 @@
         semaphores = lambda *shape: pltpu.SemaphoreType.DMA(shape)
         if jl > REACH and chips == PLANES * PLANES and my == 2 * ny and mx % (PLANES * GROUP) == 0:
             plane = chips // PLANES
-            limit = VMEM_MOST - 4 * comps * mx * jl * mz
+            limit = VMEM_MOST - 4 * (comps * (mx + nx) * jl * mz + 8 * mx)
             hbm = pl.BlockSpec(memory_space=pltpu.HBM)
-            block = pl.pallas_call(
+            block, grid, wx = pl.pallas_call(
                 functools.partial(relay, (n, comps, xl, ny, nz, jl, mz)),
-                out_shape=pltpu.VMEM((comps, mx, jl, mz), f32),
+                out_shape=(
+                    pltpu.VMEM((comps, mx, jl, mz), f32),
+                    pltpu.VMEM((comps, nx, jl, mz), f32),
+                    pltpu.VMEM((BAND, mx), f32),
+                ),
                 in_specs=[hbm] * 7,
-                out_specs=vmem,
+                out_specs=(vmem, vmem, vmem),
                 scratch_shapes=[
                     pltpu.VMEM((pairs, lanes, ny), f32),
                     pltpu.VMEM(((ny + REACH) * pairs, lanes), f32),
@@ -621,9 +672,7 @@
                     pltpu.VMEM((1, mz), jnp.int32),
                     pltpu.VMEM((BAND, mz), f32),
                     pltpu.VMEM((BAND, mx), f32),
-                    pltpu.VMEM((comps, nx, jl, mz), f32),
                     pltpu.SMEM((mx,), jnp.int32),
-                    pltpu.VMEM((BAND, mx), f32),
                     pltpu.SMEM((BAND, mx), f32),
                     semaphores(pairs),
                     semaphores(6),
@@ -637,15 +686,23 @@
                 ),
                 name="relay",
             )(slab, offsets_y, coeffs_y, offsets_z.reshape(1, mz), coeffs_z, coeffs_x, offsets_x)
+            held = lambda array: pltpu.with_memory_space_constraint(array, pltpu.VMEM)
             return pl.pallas_call(
-                store,
+                finish,
                 out_shape=jax.ShapeDtypeStruct((comps, mx, jl, mz), f32),
-                in_specs=[vmem],
-                out_specs=pl.BlockSpec(memory_space=pltpu.HBM),
-                scratch_shapes=[semaphores(comps)],
+                in_specs=[vmem, vmem, vmem, hbm],
+                out_specs=hbm,
+                scratch_shapes=[
+                    pltpu.VMEM((comps, mx, jl, mz), f32),
+                    pltpu.SMEM((mx,), jnp.int32),
+                    pltpu.SMEM((BAND, mx), f32),
+                    semaphores(comps, 2),
+                    semaphores(comps, 2),
+                    semaphores(2),
+                ],
                 compiler_params=pltpu.CompilerParams(vmem_limit_bytes=limit),
-                name="store",
-            )(pltpu.with_memory_space_constraint(block, pltpu.VMEM))
+                name="finish",
+            )(held(block), held(grid), held(wx), offsets_x)
         grid, wx = pl.pallas_call(
             functools.partial(exchange, (n, comps, xl, ny, nz, jl, mz)),
             out_shape=(

time: 24.7 us -> 24.4 us (0.988)
  Pallas kernels: 24.5 us -> 24.2 us
    pallas_call x1, Pallas kernels: 22.5 us -> 21.8 us  [body(): pl.pallas_call(functools.partial(relay, (n, comps, xl, ny, nz, jl, mz)),...]
    pallas_call x1, Pallas kernels: 2.04 us -> 2.38 us  [body(): pl.pallas_call(finish, out_shape=jax.ShapeDtypeStruct((comps, mx, jl, mz)...]
where the time goes in v3:
time: 24.4 us; the launch traced here: 24.2 us
  Pallas kernels  24.2 us (99%)
    pallas_call x1, Pallas kernels, body(): pl.pallas_call(functools.partial(relay, (n, comps, xl, ny, nz, jl, mz)),...  21.8 us
    pallas_call x1, Pallas kernels, body(): pl.pallas_call(finish, out_shape=jax.ShapeDtypeStruct((comps, mx, jl, mz)...  2.38 us

profile of v3, /device:TPU:25, one launch (start us, length us, event | category | flops | bytes accessed | tf_op | source)
XLA Modules:
  0.0 24.2 jit_solution(15964602416299525890)
XLA Ops:
  0.0 21.8 %relay.1 = (f32[4,256,8,128]{3,2,1,0:T(8,128)S(1)}, f32[4,128,8,128]{3,2,1,0:T(8,128)S(1)}, f32[4,256]{1,0:T(4,128)S(1)}) custom-call(f32[8,128,128]{2,1,0:T(8,128)} %bitcast.4, s32[256]{0:T(256)} %oy_hbm.1, f32[4,256]{1,0:T(4,128)} %cy_hbm.1, s32[1,128]{1,0:T(1,128)} %bitcast.5, f32[4,128]{1,0:T(4,128)} %cz_hbm.1, f32[4,256]{1,0:T(4,128)} %cx_hbm.1, s32[256]{0:T(256)} %ox_hbm.3), custom_call_target="tpu_custom_call" | custom-call | tf_op jit(solution)/shard_map/relay/pallas_call | solution.py:655
  21.8 2.4 %finish.1 = f32[4,256,8,128]{3,2,1,0:T(8,128)} custom-call(f32[4,256,8,128]{3,2,1,0:T(8,128)S(1)} %get-tuple-element.8.ready_ref, f32[4,128,8,128]{3,2,1,0:T(8,128)S(1)} %get-tuple-element.9.grid_ref, f32[4,256]{1,0:T(4,128)S(1)} %get-tuple-element.10.wx_hbm, s32[256]{0:T(256)} %ox_hbm.3), custom_call_target="tpu_custom_call" | custom-call | tf_op jit(solution)/shard_map/finish/pallas_call | solution.py:690

commit v4 on v3

--- a/solution.py
+++ b/solution.py
@@ -478,7 +478,6 @@
     make_weights(dims, me, span_base, oy_ref, cy_ref, oz_ref, cz_ref, cx_ref, wx_ref, wy, rz, rz_lo)
     scalars = pltpu.make_async_copy(wx_ref, wx_scalars, small_sem.at[0])
     scalars.start()
-    scalars.wait()
 
     for z, plan in enumerate(takes):
 
@@ -487,6 +486,8 @@
             known, written = set(), set()
             for step in plan:
                 if step == "x":
+                    if not written:
+                        scalars.wait()
                     across(known, written)
                 else:
                     acts[step[0]](int(step[1]))

time: 24.4 us -> 24.4 us (level)
  no operation moved by 1% of the time
where the time goes in v4:
time: 24.4 us; the launch traced here: 24.2 us
  Pallas kernels  24.2 us (99%)
    pallas_call x1, Pallas kernels, body(): pl.pallas_call(functools.partial(relay, (n, comps, xl, ny, nz, jl, mz)),...  21.8 us
    pallas_call x1, Pallas kernels, body(): pl.pallas_call(finish, out_shape=jax.ShapeDtypeStruct((comps, mx, jl, mz)...  2.38 us

profile of v4, /device:TPU:25, one launch (start us, length us, event | category | flops | bytes accessed | tf_op | source)
XLA Modules:
  0.0 24.2 jit_solution(11357162677203338545)
XLA Ops:
  0.0 21.8 %relay.1 = (f32[4,256,8,128]{3,2,1,0:T(8,128)S(1)}, f32[4,128,8,128]{3,2,1,0:T(8,128)S(1)}, f32[4,256]{1,0:T(4,128)S(1)}) custom-call(f32[8,128,128]{2,1,0:T(8,128)} %bitcast.4, s32[256]{0:T(256)} %oy_hbm.1, f32[4,256]{1,0:T(4,128)} %cy_hbm.1, s32[1,128]{1,0:T(1,128)} %bitcast.5, f32[4,128]{1,0:T(4,128)} %cz_hbm.1, f32[4,256]{1,0:T(4,128)} %cx_hbm.1, s32[256]{0:T(256)} %ox_hbm.3), custom_call_target="tpu_custom_call" | custom-call | tf_op jit(solution)/shard_map/relay/pallas_call | solution.py:656
  21.8 2.4 %finish.1 = f32[4,256,8,128]{3,2,1,0:T(8,128)} custom-call(f32[4,256,8,128]{3,2,1,0:T(8,128)S(1)} %get-tuple-element.8.ready_ref, f32[4,128,8,128]{3,2,1,0:T(8,128)S(1)} %get-tuple-element.9.grid_ref, f32[4,256]{1,0:T(4,128)S(1)} %get-tuple-element.10.wx_hbm, s32[256]{0:T(256)} %ox_hbm.3), custom_call_target="tpu_custom_call" | custom-call | tf_op jit(solution)/shard_map/finish/pallas_call | solution.py:691
